TPU v7x, 32 devices: a whole 2x2x4 slice. The times are simulated.
32 devices in a mesh: batch: 8 (over y, x, core), chan: 4 (over z).
Axes of the slice: x: 2, y: 2, z: 4, core: 2. Of those that a mesh axis runs over, the one named last changes fastest.
Arguments:
- images: bfloat16 [64, 14, 14, 4096], P('batch', None, None, 'chan'), may hold values from -12 to 12, as said below
- reduce_weight: bfloat16 [4096, 1024], P(None, 'chan'), may hold values from -0.09375 to 0.09375
- reduce_gain: float32 [1024], P('chan'), may hold values from 0.25 to 1.75
- reduce_bias: float32 [1024], P('chan'), may hold values from -0.5 to 0.5
- spatial_weight: bfloat16 [3, 3, 1024, 1024], P(None, None, None, 'chan'), may hold values from -0.0625 to 0.0625
- spatial_gain: float32 [1024], P('chan'), may hold values from 0.25 to 1.75
- spatial_bias: float32 [1024], P('chan'), may hold values from -0.5 to 0.5
- expand_weight: bfloat16 [1024, 4096], P(None, 'chan'), may hold values from -0.1875 to 0.1875
- expand_gain: float32 [4096], P('chan'), may hold values from 0.25 to 1.75
- expand_bias: float32 [4096], P('chan'), may hold values from -0.5 to 0.5
Outputs:
- block_out: bfloat16 [64, 14, 14, 4096], P('batch', None, None, 'chan')
Inputs may be any that keep to these rules, and one draw needn't show every extreme that they name: In the images, the per-channel mean and scale differ from one block of 8 images to the next.
All inputs are finite; a program needn't handle non-finite values.
Results may differ from a plain program's by a relative error of at most 0.0047.
Values may be sent and summed in bfloat16 or wider, within the bound.
No kernel may reach another device: no remote copies, remote signals or barrier semaphores. Data moves between devices by JAX's collectives and lax.ppermute only.
A program may use at most 128 MiB of HBM per device.

v0:
```python
import jax
import jax.numpy as jnp
from jax import lax
from jax.sharding import PartitionSpec as P

eps = 0.001


def totals(parts):
    return lax.psum((parts[0],), "batch")


def batch_norm(values, gain, bias, count):
    (total,) = totals((jnp.sum(values, axis=0),))
    mean = total / count
    centred = values - mean
    (spread,) = totals((jnp.sum(centred * centred, axis=0),))
    var = spread / count
    return centred * (gain / jnp.sqrt(var + eps)) + bias


def body(
    images,
    reduce_weight,
    reduce_gain,
    reduce_bias,
    spatial_weight,
    spatial_gain,
    spatial_bias,
    expand_weight,
    expand_gain,
    expand_bias,
):
    imgs, side = (images.shape[0], images.shape[1])
    rows = imgs * side * side
    count = rows * lax.axis_size("batch")
    mid_local = reduce_weight.shape[1]
    out_local = expand_weight.shape[1]
    own_rows = lax.all_to_all(reduce_weight, "chan", split_axis=0, concat_axis=1, tiled=True)
    partial_first = jnp.dot(
        images.reshape(rows, out_local), own_rows, preferred_element_type=jnp.float32
    )
    first = lax.psum_scatter(partial_first, "chan", scatter_dimension=1, tiled=True)
    act_one = jnp.maximum(batch_norm(first, reduce_gain, reduce_bias, count), 0.0).astype(
        jnp.bfloat16
    )
    act_one = act_one.reshape(imgs, side, side, mid_local)
    total = jnp.zeros((rows, mid_local), jnp.float32)
    piece = lax.all_gather(act_one, "chan", axis=3, tiled=True)
    width = piece.shape[-1]
    padded = jnp.pad(piece, ((0, 0), (1, 1), (1, 1), (0, 0)))
    for row_tap in range(3):
        for col_tap in range(3):
            window = padded[:, row_tap : row_tap + side, col_tap : col_tap + side, :].reshape(
                rows, width
            )
            block = spatial_weight[row_tap, col_tap]
            total = total + jnp.dot(window, block, preferred_element_type=jnp.float32)
    act_two = jnp.maximum(batch_norm(total, spatial_gain, spatial_bias, count), 0.0).astype(
        jnp.bfloat16
    )
    block = expand_weight
    third = jnp.dot(
        lax.all_gather(act_two, "chan", axis=1, tiled=True),
        block,
        preferred_element_type=jnp.float32,
    )
    normed = batch_norm(third, expand_gain, expand_bias, count)
    summed = normed + images.reshape(rows, out_local).astype(jnp.float32)
    return jnp.maximum(summed, 0.0).astype(jnp.bfloat16).reshape(imgs, side, side, out_local)


def solution(mesh):
    in_specs = (
        P("batch", None, None, "chan"),
        P(None, "chan"),
        P("chan"),
        P("chan"),
        P(None, None, None, "chan"),
        P("chan"),
        P("chan"),
        P(None, "chan"),
        P("chan"),
        P("chan"),
    )
    out_specs = P("batch", None, None, "chan")
    return jax.shard_map(body, mesh=mesh, in_specs=in_specs, out_specs=out_specs, check_vma=False)
```

profile of v0, /device:TPU:0, one launch (start us, length us, event | category | flops | bytes accessed | tf_op | source)
XLA Modules:
  0.0 540.0 jit_solution(18199424458085482704)
XLA Ops:
  6.5 6.5 %all-to-all-start = ((bf16[4,1024,256]{2,1,0:T(8,128)(2,1)}), bf16[4,1024,256]{2,1,0:T(8,128)(2,1)}, u32[]{:S(2)}, u32[]{:S(2)}) async-start(bf16[4,1024,256]{2,1,0:T(8,128)(2,1)} %bitcast.45), calls=%async_computation | async-start | bytes 4194304 | tf_op jit(solution)/shard_map/all_to_all | solution.py:39
  18.5 5.6 %reshape.49 = bf16[1568,1024]{1,0:T(8,128)(2,1)} reshape(bf16[8,14,14,1024]{3,2,1,0:T(8,128)(2,1)} %copy.15) | data formatting | bytes 6422528 | tf_op jit(solution)/shard_map/reshape | solution.py:41
  24.1 37.2 %all-to-all-done = bf16[4,1024,256]{2,1,0:T(8,128)(2,1)} async-done(((bf16[4,1024,256]{2,1,0:T(8,128)(2,1)}), bf16[4,1024,256]{2,1,0:T(8,128)(2,1)}, u32[]{:S(2)}, u32[]{:S(2)}) %all-to-all-start) | async-done | bytes 2097184 | tf_op jit(solution)/shard_map/all_to_all | solution.py:39
  65.3 8.8 %fusion.21 = f32[1568,1024]{1,0:T(8,128)} fusion(bf16[1568,1024]{1,0:T(8,128)(2,1)} %reshape.49, bf16[1024,1024]{0,1:T(8,128)(2,1)} %bitcast.46), kind=kOutput, calls=%fused_computation.49 | convolution fusion | flops 3288334336 | bytes 11730944 | tf_op jit(solution)/shard_map/dot_general | solution.py:40
  74.2 112.1 %reduce-scatter.2.cloned.1.call-done = f32[1568,256]{1,0:T(8,128)} async-done(((f32[1568,1024]{1,0:T(8,128)}), f32[1568,256]{1,0:T(8,128)}) %reduce-scatter.2.cloned.1.call-update) | async-done | bytes 1605648 | tf_op jit(solution)/shard_map/reduce_scatter | solution.py:43
  187.9 13.5 %psum.42 = f32[256]{0:T(256)S(1)} all-reduce(f32[256]{0:T(256)S(1)} %reduce_sum.54), channel_id=1, replica_groups=mesh['batch'=8,'chan'=4] {'batch'}, use_global_device_ids=true, to_apply=%region_2.0 | all-reduce | flops 256 | bytes 2048 | tf_op jit(solution)/shard_map/psum | solution.py:10
  203.1 11.8 %psum.43 = f32[256]{0:T(256)S(1)} all-reduce(f32[256]{0:T(256)S(1)} %multiply_reduce_fusion.2), channel_id=1, replica_groups=mesh['batch'=8,'chan'=4] {'batch'}, use_global_device_ids=true, to_apply=%region_4.0 | all-reduce | flops 256 | bytes 2048 | tf_op jit(solution)/shard_map/psum | solution.py:10
  218.0 70.6 %all-gather.3.cloned.1.call-done = bf16[8,14,14,1024]{3,2,1,0:T(8,128)(2,1)} async-done(((bf16[8,14,14,256]{3,2,1,0:T(8,128)(2,1)}), bf16[8,14,14,1024]{3,2,1,0:T(8,128)(2,1)}) %all-gather.3.cloned.1.call-update) | async-done | bytes 3211280 | tf_op jit(solution)/shard_map/all_gather | solution.py:49
  288.6 23.7 %pad_slice_fusion = (bf16[8,14,14,1024]{3,2,1,0:T(8,128)(2,1)}, bf16[8,14,14,1024]{3,2,1,0:T(8,128)(2,1)}, bf16[8,14,14,1024]{3,2,1,0:T(8,128)(2,1)}, bf16[8,14,...) fusion(bf16[8,14,14,1024]{3,2,1,0:T(8,128)(2,1)} %all-gather.3., ...), kind=kLoop, calls=%fused_computation.10 | loop fusion | bytes 28901376 | tf_op jit(solution)/shard_map/slice | solution.py:54
  312.3 5.7 %reshape.59 = bf16[1568,1024]{1,0:T(8,128)(2,1)} reshape(bf16[8,14,14,1024]{3,2,1,0:T(8,128)(2,1)} %get-tuple-element.5) | data formatting | bytes 6422528 | tf_op jit(solution)/shard_map/reshape | solution.py:54
  318.1 5.7 %reshape.52 = bf16[1568,1024]{1,0:T(8,128)(2,1)} reshape(bf16[8,14,14,1024]{3,2,1,0:T(8,128)(2,1)} %get-tuple-element.6) | data formatting | bytes 6422528 | tf_op jit(solution)/shard_map/reshape | solution.py:54
  329.4 5.7 %reshape.54 = bf16[1568,1024]{1,0:T(8,128)(2,1)} reshape(bf16[8,14,14,1024]{3,2,1,0:T(8,128)(2,1)} %get-tuple-element.8) | data formatting | bytes 6422528 | tf_op jit(solution)/shard_map/reshape | solution.py:54
  335.0 5.7 %reshape.56 = bf16[1568,1024]{1,0:T(8,128)(2,1)} reshape(bf16[8,14,14,1024]{3,2,1,0:T(8,128)(2,1)} %get-tuple-element.9) | data formatting | bytes 6422528 | tf_op jit(solution)/shard_map/reshape | solution.py:54
  352.0 5.7 %reshape.51 = bf16[1568,1024]{1,0:T(8,128)(2,1)} reshape(bf16[8,14,14,1024]{3,2,1,0:T(8,128)(2,1)} %get-tuple-element.12) | data formatting | bytes 6422528 | tf_op jit(solution)/shard_map/reshape | solution.py:54
  368.5 5.6 %reshape.55 = bf16[1568,1024]{1,0:T(8,128)(2,1)} reshape(bf16[8,14,14,1024]{3,2,1,0:T(8,128)(2,1)} %all-gather.3.cloned.1.call-done) | data formatting | bytes 6422528 | tf_op jit(solution)/shard_map/reshape | solution.py:54
  387.8 13.6 %psum.44 = f32[256]{0:T(256)S(1)} all-reduce(f32[256]{0:T(256)S(1)} %get-tuple-element.13), channel_id=1, replica_groups=mesh['batch'=8,'chan'=4] {'batch'}, use_global_device_ids=true, to_apply=%region_6.7 | all-reduce | flops 256 | bytes 2048 | tf_op jit(solution)/shard_map/psum | solution.py:10
  403.1 11.8 %psum.45 = f32[256]{0:T(256)S(1)} all-reduce(f32[256]{0:T(256)S(1)} %multiply_reduce_fusion.1), channel_id=1, replica_groups=mesh['batch'=8,'chan'=4] {'batch'}, use_global_device_ids=true, to_apply=%region_8.9 | all-reduce | flops 256 | bytes 2048 | tf_op jit(solution)/shard_map/psum | solution.py:10
  417.5 61.0 %all-gather.5.cloned.1.call-done = bf16[1568,1024]{1,0:T(8,128)(2,1)} async-done(((bf16[1568,256]{1,0:T(8,128)(2,1)}), bf16[1568,1024]{1,0:T(8,128)(2,1)}) %all-gather.5.cloned.1.call-update) | async-done | bytes 3211280 | tf_op jit(solution)/shard_map/all_gather | solution.py:64
  478.5 7.4 %fusion.20 = (f32[1024]{0:T(1024)S(1)}, f32[1568,1024]{1,0:T(8,128)}) fusion(bf16[1568,1024]{1,0:T(8,128)(2,1)} %all-gather.5.cloned.1.call-done, bf16[1024,1024]{1,0:T(8,128)(2,1)S(1)} %copy-done), kind=kOutput, calls=%fused_computation.48 | convolution fusion | flops 3289938944 | bytes 11735040 | tf_op jit(solution)/shard_map/dot_general | solution.py:63
  485.9 13.6 %psum.46 = f32[1024]{0:T(1024)S(1)} all-reduce(f32[1024]{0:T(1024)S(1)} %get-tuple-element.15), channel_id=1, replica_groups=mesh['batch'=8,'chan'=4] {'batch'}, use_global_device_ids=true, to_apply=%region_10.11 | all-reduce | flops 1024 | bytes 8192 | tf_op jit(solution)/shard_map/psum | solution.py:10
  503.1 11.8 %psum.47 = f32[1024]{0:T(1024)S(1)} all-reduce(f32[1024]{0:T(1024)S(1)} %multiply_reduce_fusion), channel_id=1, replica_groups=mesh['batch'=8,'chan'=4] {'batch'}, use_global_device_ids=true, to_apply=%region_12.13 | all-reduce | flops 1024 | bytes 8192 | tf_op jit(solution)/shard_map/psum | solution.py:10
  514.9 7.0 %maximum_convert_fusion = bf16[1568,1024]{1,0:T(8,128)(2,1)} fusion(bf16[1568,1024]{1,0:T(8,128)(2,1)} %reshape.49, f32[1568,1024]{1,0:T(8,128)} %get-tuple-element.16, f32[1024]{0:T(1024)S(1)} %copy-done.8, f32[1024]{0:T(1024)S(1)} %rsqrt_multiply_fusion, f32[1024]{0:T(1024)S(1)} %broadcast_multiply_fusion), kind=kLoop, calls=%fused_computation | loop fusion | flops 11239424 | bytes 12857344 | tf_op jit(solution)/shard_map/convert_element_type | solution.py:70
  521.8 5.6 %reshape.60 = bf16[8,14,14,1024]{3,2,1,0:T(8,128)(2,1)} reshape(bf16[1568,1024]{1,0:T(8,128)(2,1)} %maximum_convert_fusion) | data formatting | bytes 6422528 | tf_op jit(solution)/shard_map/reshape | solution.py:70
  527.5 6.0 %copy.17 = bf16[8,14,14,1024]{3,0,2,1:T(8,128)(2,1)} copy(bf16[8,14,14,1024]{3,2,1,0:T(8,128)(2,1)} %reshape.60) | data formatting | bytes 6422528 | tf_op jit(solution)/shard_map/reshape | solution.py:70
  (61 shorter events, 65.0 us)
Async XLA Ops:
  6.5 471.9 %copy-start = (bf16[1024,1024]{1,0:T(8,128)(2,1)S(1)}, bf16[1024,1024]{1,0:T(8,128)(2,1)}, u32[]{:S(2)}) copy-start(bf16[1024,1024]{1,0:T(8,128)(2,1)} %param.17) | copy-start | bytes 6291460
  6.5 54.8 %all-to-all-start = ((bf16[4,1024,256]{2,1,0:T(8,128)(2,1)}), bf16[4,1024,256]{2,1,0:T(8,128)(2,1)}, u32[]{:S(2)}, u32[]{:S(2)}) async-start(bf16[4,1024,256]{2,1,0:T(8,128)(2,1)} %bitcast.45), calls=%async_computation | async-start | bytes 4194304 | tf_op jit(solution)/shard_map/all_to_all | solution.py:39
  13.0 173.3 %reduce-scatter.2.cloned.1.call-start = ((), (), s32[]{:S(2)}) async-start(), calls=%async_computation.2 | async-start | bytes 8028160 | tf_op jit(solution)/shard_map/reduce_scatter | solution.py:43
  74.1 140.8 %copy-start.12 = (f32[256]{0:T(256)S(1)}, f32[256]{0:T(256)}, u32[]{:S(2)}) copy-start(f32[256]{0:T(256)} %param.12) | copy-start | bytes 3076
  74.1 140.8 %copy-start.10 = (f32[256]{0:T(256)S(1)}, f32[256]{0:T(256)}, u32[]{:S(2)}) copy-start(f32[256]{0:T(256)} %param.13) | copy-start | bytes 3076
  74.2 214.5 %all-gather.3.cloned.1.call-start = ((), (), s32[]{:S(2)}) async-start(), calls=%async_computation.3 | async-start | bytes 4587520 | tf_op jit(solution)/shard_map/all_gather | solution.py:49
  217.8 260.7 %all-gather.5.cloned.1.call-start = ((), (), s32[]{:S(2)}) async-start(), calls=%async_computation.4 | async-start | bytes 4014080 | tf_op jit(solution)/shard_map/all_gather | solution.py:64
  357.6 3.2 copy-start.7
  360.8 2.2 copy-start.6
  363.0 2.2 copy-start.5
  374.2 3.7 copy-start.4
  377.9 2.2 copy-start.3
  380.1 2.2 copy-start.2
  382.3 2.2 copy-start.1
  384.5 30.4 %copy-start.13 = (f32[256]{0:T(256)S(1)}, f32[256]{0:T(256)}, u32[]{:S(2)}) copy-start(f32[256]{0:T(256)} %param.15) | copy-start | bytes 3076
  384.6 30.4 %copy-start.11 = (f32[256]{0:T(256)S(1)}, f32[256]{0:T(256)}, u32[]{:S(2)}) copy-start(f32[256]{0:T(256)} %param.16) | copy-start | bytes 3076
  499.5 15.4 %copy-start.9 = (f32[1024]{0:T(1024)S(1)}, f32[1024]{0:T(1024)}, u32[]{:S(2)}) copy-start(f32[1024]{0:T(1024)} %param.18) | copy-start | bytes 12292
  499.5 15.4 %copy-start.8 = (f32[1024]{0:T(1024)S(1)}, f32[1024]{0:T(1024)}, u32[]{:S(2)}) copy-start(f32[1024]{0:T(1024)} %param.19) | copy-start | bytes 12292
Sparse Core Ops, SparseCore 0:
  74.3 111.9 reduce-scatter.1
  217.9 70.6 all-gather.2
  417.6 60.7 all-gather.4
where the time goes:
time: 542 us; the launch traced here: 540 us
  waiting for transfers between devices  281 us (52%)
  local copies, waits for them, and re-layouts  103 us (19%)
  blocking collectives  76.2 us (14%)
  matrix products  40.5 us (7%)
  other arithmetic  19.7 us (4%)
  between operations  13.3 us (2%)
  starting transfers between devices  6.74 us (1%)
    reduce_scatter x1, waiting for transfers between devices, body(): lax.psum_scatter(partial_first, 'chan', scatter_dimension=1, tiled=True)  112 us
    psum x6, blocking collectives, totals(): return lax.psum((parts[0],), 'batch')  76.2 us
    all_gather x1, waiting for transfers between devices, body(): piece = lax.all_gather(act_one, 'chan', axis=3, tiled=True)  70.6 us
    all_gather x1, waiting for transfers between devices, body(): lax.all_gather(act_two, 'chan', axis=1, tiled=True)  61 us
    reshape x9, local copies, waits for them, and re-layouts, body(): padded[:, row_tap:row_tap + side, col_tap:col_tap + side, :]  50.9 us
    all_to_all x1, waiting for transfers between devices, body(): lax.all_to_all(reduce_weight, 'chan', split_axis=0, concat_axis=1, tiled=...  37.2 us
    dot_general x9, matrix products, body(): total = total + jnp.dot(window, block, preferred_element_type=jnp.float32)  24.4 us
    slice x1, local copies, waits for them, and re-layouts, body(): padded[:, row_tap:row_tap + side, col_tap:col_tap + side, :]  23.7 us
  transfers between devices with their start and end apart: 4, of which 4 were waited for; matrix products, arithmetic and copies ran while one was open for 2% of the time, Pallas kernels for 0%

commit v1 on v0

--- a/solution.py
+++ b/solution.py
@@ -36,7 +36,10 @@
     count = rows * lax.axis_size("batch")
     mid_local = reduce_weight.shape[1]
     out_local = expand_weight.shape[1]
-    own_rows = lax.all_to_all(reduce_weight, "chan", split_axis=0, concat_axis=1, tiled=True)
+    size = lax.axis_size("chan")
+    blocks = jnp.stack(jnp.split(reduce_weight, size, axis=0), axis=0)
+    blocks = lax.all_to_all(blocks, "chan", split_axis=0, concat_axis=0)
+    own_rows = jnp.concatenate(blocks, axis=1)
     partial_first = jnp.dot(
         images.reshape(rows, out_local), own_rows, preferred_element_type=jnp.float32
     )

time: 542 us -> 550 us (1.015)
    unnamed x29 -> x33, local copies, waits for them, and re-layouts: 5.56 us -> 11.9 us
where the time goes in v1:
time: 550 us; the launch traced here: 548 us
  waiting for transfers between devices  281 us (51%)
  local copies, waits for them, and re-layouts  108 us (20%)
  blocking collectives  76.2 us (14%)
  matrix products  40.5 us (7%)
  other arithmetic  22.7 us (4%)
  between operations  13.4 us (2%)
  starting transfers between devices  6.61 us (1%)
    reduce_scatter x1, waiting for transfers between devices, body(): lax.psum_scatter(partial_first, 'chan', scatter_dimension=1, tiled=True)  112 us
    psum x6, blocking collectives, totals(): return lax.psum((parts[0],), 'batch')  76.2 us
    all_gather x1, waiting for transfers between devices, body(): piece = lax.all_gather(act_one, 'chan', axis=3, tiled=True)  70.5 us
    all_gather x1, waiting for transfers between devices, body(): lax.all_gather(act_two, 'chan', axis=1, tiled=True)  60.9 us
    reshape x9, local copies, waits for them, and re-layouts, body(): padded[:, row_tap:row_tap + side, col_tap:col_tap + side, :]  50.9 us
    all_to_all x1, waiting for transfers between devices, body(): blocks = lax.all_to_all(blocks, 'chan', split_axis=0, concat_axis=0)  37.2 us
    dot_general x9, matrix products, body(): total = total + jnp.dot(window, block, preferred_element_type=jnp.float32)  24.4 us
    slice x1, local copies, waits for them, and re-layouts, body(): padded[:, row_tap:row_tap + side, col_tap:col_tap + side, :]  23.7 us
  transfers between devices with their start and end apart: 4, of which 4 were waited for; matrix products, arithmetic and copies ran while one was open for 2% of the time, Pallas kernels for 0%

profile of v1, /device:TPU:0, one launch (start us, length us, event | category | flops | bytes accessed | tf_op | source)
XLA Modules:
  0.0 548.0 jit_solution(7141727104929392728)
XLA Ops:
  18.7 6.3 %all-to-all-start = ((bf16[4,1024,256]{1,2,0:T(8,128)(2,1)}), bf16[4,1024,256]{1,2,0:T(8,128)(2,1)}, u32[]{:S(2)}, u32[]{:S(2)}) async-start(bf16[4,1024,256]{1,2,0:T(8,128)(2,1)} %pad_maximum_fusion), calls=%async_computation | async-start | bytes 4194304 | tf_op jit(solution)/shard_map/all_to_all | solution.py:41
  30.5 5.6 %reshape.54 = bf16[1568,1024]{1,0:T(8,128)(2,1)} reshape(bf16[8,14,14,1024]{3,2,1,0:T(8,128)(2,1)} %copy.17) | data formatting | bytes 6422528 | tf_op jit(solution)/shard_map/reshape | solution.py:44
  36.2 37.2 %all-to-all-done = bf16[4,1024,256]{1,2,0:T(8,128)(2,1)} async-done(((bf16[4,1024,256]{1,2,0:T(8,128)(2,1)}), bf16[4,1024,256]{1,2,0:T(8,128)(2,1)}, u32[]{:S(2)}, u32[]{:S(2)}) %all-to-all-start) | async-done | bytes 2097184 | tf_op jit(solution)/shard_map/all_to_all | solution.py:41
  73.4 8.8 %convolution_bitcast_fusion = f32[1568,1024]{1,0:T(8,128)} fusion(bf16[1024,1024]{0,1:T(8,128)(2,1)} %bitcast.5, bf16[1568,1024]{1,0:T(8,128)(2,1)} %reshape.54), kind=kOutput, calls=%fused_computation.2 | convolution fusion | flops 3288334336 | bytes 11730944 | tf_op jit(solution)/shard_map/dot_general | solution.py:43
  82.2 112.1 %reduce-scatter.2.cloned.1.call-done = f32[1568,256]{1,0:T(8,128)} async-done(((f32[1568,1024]{1,0:T(8,128)}), f32[1568,256]{1,0:T(8,128)}) %reduce-scatter.2.cloned.1.call-update) | async-done | bytes 1605648 | tf_op jit(solution)/shard_map/reduce_scatter | solution.py:46
  195.9 13.6 %psum.42 = f32[256]{0:T(256)S(1)} all-reduce(f32[256]{0:T(256)S(1)} %reduce_sum.54), channel_id=1, replica_groups=mesh['batch'=8,'chan'=4] {'batch'}, use_global_device_ids=true, to_apply=%region_2.0 | all-reduce | flops 256 | bytes 2048 | tf_op jit(solution)/shard_map/psum | solution.py:10
  211.2 11.8 %psum.43 = f32[256]{0:T(256)S(1)} all-reduce(f32[256]{0:T(256)S(1)} %multiply_reduce_fusion.2), channel_id=1, replica_groups=mesh['batch'=8,'chan'=4] {'batch'}, use_global_device_ids=true, to_apply=%region_4.0 | all-reduce | flops 256 | bytes 2048 | tf_op jit(solution)/shard_map/psum | solution.py:10
  226.1 70.5 %all-gather.3.cloned.1.call-done = bf16[8,14,14,1024]{3,2,1,0:T(8,128)(2,1)} async-done(((bf16[8,14,14,256]{3,2,1,0:T(8,128)(2,1)}), bf16[8,14,14,1024]{3,2,1,0:T(8,128)(2,1)}) %all-gather.3.cloned.1.call-update) | async-done | bytes 3211280 | tf_op jit(solution)/shard_map/all_gather | solution.py:52
  296.6 23.7 %pad_slice_fusion = (bf16[8,14,14,1024]{3,2,1,0:T(8,128)(2,1)}, bf16[8,14,14,1024]{3,2,1,0:T(8,128)(2,1)}, bf16[8,14,14,1024]{3,2,1,0:T(8,128)(2,1)}, bf16[8,14,...) fusion(bf16[8,14,14,1024]{3,2,1,0:T(8,128)(2,1)} %all-gather.3., ...), kind=kLoop, calls=%fused_computation.11 | loop fusion | bytes 28901376 | tf_op jit(solution)/shard_map/slice | solution.py:57
  320.4 5.7 %reshape.64 = bf16[1568,1024]{1,0:T(8,128)(2,1)} reshape(bf16[8,14,14,1024]{3,2,1,0:T(8,128)(2,1)} %get-tuple-element.5) | data formatting | bytes 6422528 | tf_op jit(solution)/shard_map/reshape | solution.py:57
  326.1 5.7 %reshape.57 = bf16[1568,1024]{1,0:T(8,128)(2,1)} reshape(bf16[8,14,14,1024]{3,2,1,0:T(8,128)(2,1)} %get-tuple-element.6) | data formatting | bytes 6422528 | tf_op jit(solution)/shard_map/reshape | solution.py:57
  337.4 5.7 %reshape.59 = bf16[1568,1024]{1,0:T(8,128)(2,1)} reshape(bf16[8,14,14,1024]{3,2,1,0:T(8,128)(2,1)} %get-tuple-element.8) | data formatting | bytes 6422528 | tf_op jit(solution)/shard_map/reshape | solution.py:57
  343.1 5.7 %reshape.61 = bf16[1568,1024]{1,0:T(8,128)(2,1)} reshape(bf16[8,14,14,1024]{3,2,1,0:T(8,128)(2,1)} %get-tuple-element.9) | data formatting | bytes 6422528 | tf_op jit(solution)/shard_map/reshape | solution.py:57
  360.0 5.7 %reshape.56 = bf16[1568,1024]{1,0:T(8,128)(2,1)} reshape(bf16[8,14,14,1024]{3,2,1,0:T(8,128)(2,1)} %get-tuple-element.12) | data formatting | bytes 6422528 | tf_op jit(solution)/shard_map/reshape | solution.py:57
  376.5 5.6 %reshape.60 = bf16[1568,1024]{1,0:T(8,128)(2,1)} reshape(bf16[8,14,14,1024]{3,2,1,0:T(8,128)(2,1)} %all-gather.3.cloned.1.call-done) | data formatting | bytes 6422528 | tf_op jit(solution)/shard_map/reshape | solution.py:57
  395.8 13.6 %psum.44 = f32[256]{0:T(256)S(1)} all-reduce(f32[256]{0:T(256)S(1)} %get-tuple-element.17), channel_id=1, replica_groups=mesh['batch'=8,'chan'=4] {'batch'}, use_global_device_ids=true, to_apply=%region_6.7 | all-reduce | flops 256 | bytes 2048 | tf_op jit(solution)/shard_map/psum | solution.py:10
  411.2 11.8 %psum.45 = f32[256]{0:T(256)S(1)} all-reduce(f32[256]{0:T(256)S(1)} %multiply_reduce_fusion.1), channel_id=1, replica_groups=mesh['batch'=8,'chan'=4] {'batch'}, use_global_device_ids=true, to_apply=%region_8.9 | all-reduce | flops 256 | bytes 2048 | tf_op jit(solution)/shard_map/psum | solution.py:10
  425.5 60.9 %all-gather.5.cloned.1.call-done = bf16[1568,1024]{1,0:T(8,128)(2,1)} async-done(((bf16[1568,256]{1,0:T(8,128)(2,1)}), bf16[1568,1024]{1,0:T(8,128)(2,1)}) %all-gather.5.cloned.1.call-update) | async-done | bytes 3211280 | tf_op jit(solution)/shard_map/all_gather | solution.py:67
  486.5 7.4 %fusion.21 = (f32[1024]{0:T(1024)S(1)}, f32[1568,1024]{1,0:T(8,128)}) fusion(bf16[1568,1024]{1,0:T(8,128)(2,1)} %all-gather.5.cloned.1.call-done, bf16[1024,1024]{1,0:T(8,128)(2,1)S(1)} %copy-done), kind=kOutput, calls=%fused_computation.51 | convolution fusion | flops 3289938944 | bytes 11735040 | tf_op jit(solution)/shard_map/dot_general | solution.py:66
  493.9 13.6 %psum.46 = f32[1024]{0:T(1024)S(1)} all-reduce(f32[1024]{0:T(1024)S(1)} %get-tuple-element.19), channel_id=1, replica_groups=mesh['batch'=8,'chan'=4] {'batch'}, use_global_device_ids=true, to_apply=%region_10.11 | all-reduce | flops 1024 | bytes 8192 | tf_op jit(solution)/shard_map/psum | solution.py:10
  511.1 11.8 %psum.47 = f32[1024]{0:T(1024)S(1)} all-reduce(f32[1024]{0:T(1024)S(1)} %multiply_reduce_fusion), channel_id=1, replica_groups=mesh['batch'=8,'chan'=4] {'batch'}, use_global_device_ids=true, to_apply=%region_12.13 | all-reduce | flops 1024 | bytes 8192 | tf_op jit(solution)/shard_map/psum | solution.py:10
  522.9 7.0 %maximum_convert_fusion = bf16[1568,1024]{1,0:T(8,128)(2,1)} fusion(bf16[1568,1024]{1,0:T(8,128)(2,1)} %reshape.54, f32[1568,1024]{1,0:T(8,128)} %get-tuple-element.20, f32[1024]{0:T(1024)S(1)} %copy-done.8, f32[1024]{0:T(1024)S(1)} %rsqrt_multiply_fusion, f32[1024]{0:T(1024)S(1)} %broadcast_multiply_fusion), kind=kLoop, calls=%fused_computation | loop fusion | flops 11239424 | bytes 12857344 | tf_op jit(solution)/shard_map/convert_element_type | solution.py:73
  529.8 5.6 %reshape.65 = bf16[8,14,14,1024]{3,2,1,0:T(8,128)(2,1)} reshape(bf16[1568,1024]{1,0:T(8,128)(2,1)} %maximum_convert_fusion) | data formatting | bytes 6422528 | tf_op jit(solution)/shard_map/reshape | solution.py:73
  535.5 6.0 %copy.18 = bf16[8,14,14,1024]{3,0,2,1:T(8,128)(2,1)} copy(bf16[8,14,14,1024]{3,2,1,0:T(8,128)(2,1)} %reshape.65) | data formatting | bytes 6422528 | tf_op jit(solution)/shard_map/reshape | solution.py:73
  (66 shorter events, 73.2 us)
Async XLA Ops:
  6.5 480.0 %copy-start = (bf16[1024,1024]{1,0:T(8,128)(2,1)S(1)}, bf16[1024,1024]{1,0:T(8,128)(2,1)}, u32[]{:S(2)}) copy-start(bf16[1024,1024]{1,0:T(8,128)(2,1)} %param.17) | copy-start | bytes 6291460
  18.7 54.6 %all-to-all-start = ((bf16[4,1024,256]{1,2,0:T(8,128)(2,1)}), bf16[4,1024,256]{1,2,0:T(8,128)(2,1)}, u32[]{:S(2)}, u32[]{:S(2)}) async-start(bf16[4,1024,256]{1,2,0:T(8,128)(2,1)} %pad_maximum_fusion), calls=%async_computation | async-start | bytes 4194304 | tf_op jit(solution)/shard_map/all_to_all | solution.py:41
  25.1 169.3 %reduce-scatter.2.cloned.1.call-start = ((), (), s32[]{:S(2)}) async-start(), calls=%async_computation.2 | async-start | bytes 8028160 | tf_op jit(solution)/shard_map/reduce_scatter | solution.py:46
  82.2 140.9 %copy-start.12 = (f32[256]{0:T(256)S(1)}, f32[256]{0:T(256)}, u32[]{:S(2)}) copy-start(f32[256]{0:T(256)} %param.12) | copy-start | bytes 3076
  82.2 140.8 %copy-start.10 = (f32[256]{0:T(256)S(1)}, f32[256]{0:T(256)}, u32[]{:S(2)}) copy-start(f32[256]{0:T(256)} %param.13) | copy-start | bytes 3076
  82.2 214.4 %all-gather.3.cloned.1.call-start = ((), (), s32[]{:S(2)}) async-start(), calls=%async_computation.3 | async-start | bytes 4587520 | tf_op jit(solution)/shard_map/all_gather | solution.py:52
  225.9 260.6 %all-gather.5.cloned.1.call-start = ((), (), s32[]{:S(2)}) async-start(), calls=%async_computation.4 | async-start | bytes 4014080 | tf_op jit(solution)/shard_map/all_gather | solution.py:67
  365.6 3.2 copy-start.7
  368.8 2.2 copy-start.6
  371.0 2.2 copy-start.5
  382.2 3.7 copy-start.4
  385.9 2.2 copy-start.3
  388.1 2.2 copy-start.2
  390.3 2.2 copy-start.1
  392.6 30.4 %copy-start.13 = (f32[256]{0:T(256)S(1)}, f32[256]{0:T(256)}, u32[]{:S(2)}) copy-start(f32[256]{0:T(256)} %param.15) | copy-start | bytes 3076
  392.6 30.4 %copy-start.11 = (f32[256]{0:T(256)S(1)}, f32[256]{0:T(256)}, u32[]{:S(2)}) copy-start(f32[256]{0:T(256)} %param.16) | copy-start | bytes 3076
  507.5 15.4 %copy-start.9 = (f32[1024]{0:T(1024)S(1)}, f32[1024]{0:T(1024)}, u32[]{:S(2)}) copy-start(f32[1024]{0:T(1024)} %param.18) | copy-start | bytes 12292
  507.5 15.4 %copy-start.8 = (f32[1024]{0:T(1024)S(1)}, f32[1024]{0:T(1024)}, u32[]{:S(2)}) copy-start(f32[1024]{0:T(1024)} %param.19) | copy-start | bytes 12292
Sparse Core Ops, SparseCore 0:
  82.3 111.9 reduce-scatter.1
  226.0 70.5 all-gather.2
  425.7 60.7 all-gather.4
